TPU v7x, 256 devices: a whole 4x4x8 slice. The times are simulated.
256 devices in a mesh: fsdp: 16 (over y, z_lo, core), sp: 16 (over x, z_hi).
Axes of the slice: x: 4, y: 4, z: 8 (z_hi: 4, z_lo: 2; z = z_hi * 2 + z_lo), core: 2. Of those that a mesh axis runs over, the one named last changes fastest.
Arguments:
- hidden: bfloat16 [16, 4096, 5120], P('fsdp', 'sp'), may hold values from -6 to 6
- queries: bfloat16 [16, 4096, 4096], P('fsdp', 'sp'), may hold values from -240 to 240
- norm_gain: float32 [5120], replicated, may hold values from 0.5 to 1.5
- kv_weight: bfloat16 [5120, 2048], P('fsdp'), may hold values from -0.078125 to 0.078125
- value_bias: float32 [1024], replicated, may hold values from -3 to 3
- doc_lengths: int32 [16, 16], P('fsdp'), may hold values from 1 to 1024, 4096 in all within a row
Outputs:
- attended: bfloat16 [16, 4096, 4096], P('fsdp', 'sp')
Inputs may be any that keep to these rules, and one draw needn't show every extreme that they name: `doc_lengths`: each row sums to 4096 and its largest entry is 1024.
All inputs are finite; a program needn't handle non-finite values.
Results may differ from a plain program's by a relative error of at most 0.0067.
Values may be sent and summed in bfloat16 or wider, within the bound.
A program may use at most 128 MiB of HBM per device.

v0:
```python
import jax
import jax.numpy as jnp
from jax import lax
from jax.sharding import PartitionSpec as P

QH = 32
KVH = 8
HD = 128
EPS = 1e-06


def from_behind(value, axis, by):
    count = lax.axis_size(axis)
    pairs = [(i, i + by) for i in range(count) if 0 <= i + by < count]
    return lax.ppermute(value, axis, pairs)


def attend_near(query_rows, key_all, value_all, query_pos, key_pos, query_ids, key_ids):
    token_count = query_rows.shape[0]
    ratio = QH // KVH
    scale = HD ** (-0.5)
    allowed = (
        (key_pos[None, :] >= 0)
        & (key_pos[None, :] <= query_pos[:, None])
        & (key_ids[None, :] == query_ids[:, None])
    )
    query_groups = jnp.transpose(query_rows.reshape(token_count, KVH, ratio, HD), (1, 0, 2, 3))
    key_groups = jnp.transpose(key_all, (1, 0, 2))
    value_groups = jnp.transpose(value_all, (1, 0, 2))

    def one_group(operands):
        query_one, key_one, value_one = operands
        scores = (
            jnp.einsum("qrd,kd->rqk", query_one, key_one, preferred_element_type=jnp.float32)
            * scale
        )
        scores = jnp.where(allowed[None], scores, -jnp.inf)
        highest = jnp.max(scores, axis=-1, keepdims=True)
        probs = jnp.exp(scores - highest)
        probs = (probs / jnp.sum(probs, axis=-1, keepdims=True)).astype(jnp.bfloat16)
        output = jnp.einsum("rqk,kd->qrd", probs, value_one, preferred_element_type=jnp.float32)
        return output.astype(jnp.bfloat16)

    outputs = lax.map(one_group, (query_groups, key_groups, value_groups))
    return jnp.transpose(outputs, (1, 0, 2, 3)).reshape(token_count, QH * HD)


def shards(hidden, queries, norm_gain, kv_weight, value_bias, doc_lengths):
    token_count = hidden.shape[1]
    group_size = lax.axis_size("sp")
    query_rows = queries[0]
    wide = hidden[0].astype(jnp.float32)
    normed = (
        wide * lax.rsqrt(jnp.mean(wide * wide, axis=-1, keepdims=True) + EPS) * norm_gain
    ).astype(jnp.bfloat16)
    projected = jnp.dot(
        normed,
        lax.all_gather(kv_weight, "fsdp", axis=0, tiled=True),
        preferred_element_type=jnp.float32,
    )
    keys = projected[:, : KVH * HD].astype(jnp.bfloat16).reshape(token_count, KVH, HD)
    values = (
        (projected[:, KVH * HD :] + value_bias).astype(jnp.bfloat16).reshape(token_count, KVH, HD)
    )
    ends = jnp.cumsum(doc_lengths[0])
    reach = group_size // 4
    first = lax.axis_index("sp") * token_count
    key_parts = [keys]
    value_parts = [values]
    for back in range(1, reach + 1):
        key_far, value_far = from_behind((keys, values), "sp", back)
        key_parts.insert(0, key_far)
        value_parts.insert(0, value_far)
    key_all = jnp.concatenate(key_parts, axis=0)
    value_all = jnp.concatenate(value_parts, axis=0)
    query_pos = first + jnp.arange(token_count, dtype=jnp.int32)
    key_pos = first - reach * token_count + jnp.arange(key_all.shape[0], dtype=jnp.int32)
    query_ids = jnp.sum((query_pos[:, None] >= ends[None, :]).astype(jnp.int32), axis=1)
    key_ids = jnp.sum((key_pos[:, None] >= ends[None, :]).astype(jnp.int32), axis=1)
    result = attend_near(query_rows, key_all, value_all, query_pos, key_pos, query_ids, key_ids)
    return result.reshape(1, token_count, QH * HD)


def solution(mesh):
    in_specs = (
        P("fsdp", "sp", None),
        P("fsdp", "sp", None),
        P(),
        P("fsdp", None),
        P(),
        P("fsdp", None),
    )
    out_specs = P("fsdp", "sp", None)
    return jax.shard_map(shards, mesh=mesh, in_specs=in_specs, out_specs=out_specs, check_vma=False)
```

profile of v0, /device:TPU:135, one launch (start us, length us, event | category | flops | bytes accessed | tf_op | source)
XLA Modules:
  0.0 336.2 jit_solution(246101491837138390)
XLA Ops:
  8.3 2.3 fusion.50
  10.7 114.0 %all-gather.2.cloned.1.call-done = bf16[5120,2048]{1,0:T(8,128)(2,1)} async-done(((bf16[320,2048]{1,0:T(8,128)(2,1)}), bf16[5120,2048]{1,0:T(8,128)(2,1)}) %all-gather.2.cloned.1.call-update) | async-done | bytes 20971536 | tf_op jit(solution)/shard_map/all_gather | solution.py:58
  124.7 9.9 %fusion.53 = f32[256,2048]{1,0:T(8,128)S(1)} fusion(bf16[5120,2048]{1,0:T(8,128)(2,1)} %all-gather.2.cloned.1.call-done, bf16[1,256,5120]{2,1,0:T(8,128)(2,1)S(1)} %copy-done, f32[5120]{0:T(1024)S(1)} %copy-done.6, f32[256]{0:T(256)S(1)} %add_rsqrt_fusion), kind=kOutput, calls=%fused_computation.37 | convolution fusion | flops 5373952000 | bytes 25711616 | tf_op jit(solution)/shard_map/dot_general | solution.py:56
  134.6 1.3 copy-done.1
  136.3 1.4 collective-permute-start
  137.7 1.3 collective-permute-start.1
  140.4 4.1 %copy.46 = bf16[1,256,4096]{1,2,0:T(8,128)(2,1)} copy(bf16[1,256,4096]{2,1,0:T(8,128)(2,1)} %param.9) | data formatting | bytes 4194304 | tf_op args[1]
  144.5 2.4 collective-permute-start.3
  148.3 5.8 %collective-permute-done = bf16[256,8,128]{0,2,1:T(8,128)(2,1)} collective-permute-done((bf16[256,8,128]{0,2,1:T(8,128)(2,1)S(1)}, bf16[256,8,128]{0,2,1:T(8,128)(2,1)}, u32[]{:S(2)}, u32[]{:S(2)}) %collective-permute-start) | collective-permute-done | bytes 524320 | tf_op jit(solution)/shard_map/ppermute | solution.py:15
  156.4 35.8 %collective-permute-done.1 = bf16[256,8,128]{0,2,1:T(8,128)(2,1)} collective-permute-done((bf16[256,8,128]{0,2,1:T(8,128)(2,1)S(1)}, bf16[256,8,128]{0,2,1:T(8,128)(2,1)}, u32[]{:S(2)}, u32[]{:S(2)}) %collective-permute-start.1) | collective-permute-done | bytes 524320 | tf_op jit(solution)/shard_map/ppermute | solution.py:15
  194.6 32.9 %collective-permute-start.7 = (bf16[256,8,128]{2,0,1:T(8,128)(2,1)S(1)}, bf16[256,8,128]{2,0,1:T(8,128)(2,1)S(1)}, u32[]{:S(2)}, u32[]{:S(2)}) collective-permute-start(bf16[256,8,128]{2,0,1:T(8,128)(2,1)S(1)} %copy_bitcast_fusion), channel_id=1, source_target_pairs={{0,1},{1,2},{2,3},{3,4},{4,5},{5,6},{6,7},{7,8},{8,9},{9,10},{10,1... | collective-permute-start | bytes 1572872 | tf_op jit(solution)/shard_map/ppermute | solution.py:15
  228.9 6.2 %collective-permute-done.6 = bf16[256,8,128]{2,0,1:T(8,128)(2,1)S(1)} collective-permute-done((bf16[256,8,128]{2,0,1:T(8,128)(2,1)S(1)}, bf16[256,8,128]{2,0,1:T(8,128)(2,1)S(1)}, u32[]{:S(2)}, u32[]{:S(2)}) %collective-permute-start.6) | collective-permute-done | bytes 524320 | tf_op jit(solution)/shard_map/ppermute | solution.py:15
  235.2 23.7 %collective-permute-done.7 = bf16[256,8,128]{2,0,1:T(8,128)(2,1)S(1)} collective-permute-done((bf16[256,8,128]{2,0,1:T(8,128)(2,1)S(1)}, bf16[256,8,128]{2,0,1:T(8,128)(2,1)S(1)}, u32[]{:S(2)}, u32[]{:S(2)}) %collective-permute-start.7) | collective-permute-done | bytes 524320 | tf_op jit(solution)/shard_map/ppermute | solution.py:15
  259.1 1.5 copy-done.4
  260.6 64.7 %while.11 = (s32[]{:T(128)}, bf16[8,256,4,128]{1,3,2,0:T(8,128)(2,1)}, bf16[8,1280,128]{1,2,0:T(8,128)(2,1)}, bf16[8,1280,128]{2,1,0:T(8,128)(2,1)}, bf16[8,256,...) while((s32[]{:T(128)}, ...), condition=%wide.region_7.8_spmd.clone, body=%wide.region_4.7_spmd.clone.sunk | while | flops 1019874816 | bytes 2777453 | solution.py:44
  261.6 2.9 exponential_reduce_fusion.2
  264.5 4.2 %fusion.78 = bf16[8,256,4,128]{1,3,2,0:T(8,128)(2,1)} fusion(bf16[8,256,4,128]{1,3,2,0:T(8,128)(2,1)} %get-tuple-element.178, s32[]{:T(128)} %get-tuple-element.177, f32[4,256]{1,0:T(4,128)S(1)} %exponential_reduce_fusion.2, bf16[8,1280,128]{1,2,0:T(8,128)(2,1)} %get-tuple-element.190, pred[256,1280]{0,1:T(8,128)(4,1)S(1)} %compare_and_fusion.2, ...), kind=kOutput, calls=%fused_computation.10.clone.1 | convolution fusion | flops 677775616 | bytes 1513472 | tf_op jit(solution)/shard_map/while/body/eval_jaxpr/rqk,kd->qrd/dot_general | solution.py:41
  269.7 2.9 exponential_reduce_fusion.2
  272.6 4.1 %fusion.78 = bf16[8,256,4,128]{1,3,2,0:T(8,128)(2,1)} fusion(bf16[8,256,4,128]{1,3,2,0:T(8,128)(2,1)} %get-tuple-element.178, s32[]{:T(128)} %get-tuple-element.177, f32[4,256]{1,0:T(4,128)S(1)} %exponential_reduce_fusion.2, bf16[8,1280,128]{1,2,0:T(8,128)(2,1)} %get-tuple-element.190, pred[256,1280]{0,1:T(8,128)(4,1)S(1)} %compare_and_fusion.2, ...), kind=kOutput, calls=%fused_computation.10.clone.1 | convolution fusion | flops 677775616 | bytes 1513472 | tf_op jit(solution)/shard_map/while/body/eval_jaxpr/rqk,kd->qrd/dot_general | solution.py:41
  277.8 2.9 exponential_reduce_fusion.2
  280.6 4.1 %fusion.78 = bf16[8,256,4,128]{1,3,2,0:T(8,128)(2,1)} fusion(bf16[8,256,4,128]{1,3,2,0:T(8,128)(2,1)} %get-tuple-element.178, s32[]{:T(128)} %get-tuple-element.177, f32[4,256]{1,0:T(4,128)S(1)} %exponential_reduce_fusion.2, bf16[8,1280,128]{1,2,0:T(8,128)(2,1)} %get-tuple-element.190, pred[256,1280]{0,1:T(8,128)(4,1)S(1)} %compare_and_fusion.2, ...), kind=kOutput, calls=%fused_computation.10.clone.1 | convolution fusion | flops 677775616 | bytes 1513472 | tf_op jit(solution)/shard_map/while/body/eval_jaxpr/rqk,kd->qrd/dot_general | solution.py:41
  285.8 2.9 exponential_reduce_fusion.2
  288.7 4.2 %fusion.78 = bf16[8,256,4,128]{1,3,2,0:T(8,128)(2,1)} fusion(bf16[8,256,4,128]{1,3,2,0:T(8,128)(2,1)} %get-tuple-element.178, s32[]{:T(128)} %get-tuple-element.177, f32[4,256]{1,0:T(4,128)S(1)} %exponential_reduce_fusion.2, bf16[8,1280,128]{1,2,0:T(8,128)(2,1)} %get-tuple-element.190, pred[256,1280]{0,1:T(8,128)(4,1)S(1)} %compare_and_fusion.2, ...), kind=kOutput, calls=%fused_computation.10.clone.1 | convolution fusion | flops 677775616 | bytes 1513472 | tf_op jit(solution)/shard_map/while/body/eval_jaxpr/rqk,kd->qrd/dot_general | solution.py:41
  293.9 2.9 exponential_reduce_fusion.2
  296.8 4.2 %fusion.78 = bf16[8,256,4,128]{1,3,2,0:T(8,128)(2,1)} fusion(bf16[8,256,4,128]{1,3,2,0:T(8,128)(2,1)} %get-tuple-element.178, s32[]{:T(128)} %get-tuple-element.177, f32[4,256]{1,0:T(4,128)S(1)} %exponential_reduce_fusion.2, bf16[8,1280,128]{1,2,0:T(8,128)(2,1)} %get-tuple-element.190, pred[256,1280]{0,1:T(8,128)(4,1)S(1)} %compare_and_fusion.2, ...), kind=kOutput, calls=%fused_computation.10.clone.1 | convolution fusion | flops 677775616 | bytes 1513472 | tf_op jit(solution)/shard_map/while/body/eval_jaxpr/rqk,kd->qrd/dot_general | solution.py:41
  302.0 2.9 exponential_reduce_fusion.2
  304.9 4.2 %fusion.78 = bf16[8,256,4,128]{1,3,2,0:T(8,128)(2,1)} fusion(bf16[8,256,4,128]{1,3,2,0:T(8,128)(2,1)} %get-tuple-element.178, s32[]{:T(128)} %get-tuple-element.177, f32[4,256]{1,0:T(4,128)S(1)} %exponential_reduce_fusion.2, bf16[8,1280,128]{1,2,0:T(8,128)(2,1)} %get-tuple-element.190, pred[256,1280]{0,1:T(8,128)(4,1)S(1)} %compare_and_fusion.2, ...), kind=kOutput, calls=%fused_computation.10.clone.1 | convolution fusion | flops 677775616 | bytes 1513472 | tf_op jit(solution)/shard_map/while/body/eval_jaxpr/rqk,kd->qrd/dot_general | solution.py:41
  310.1 2.9 exponential_reduce_fusion.2
  313.0 4.2 %fusion.78 = bf16[8,256,4,128]{1,3,2,0:T(8,128)(2,1)} fusion(bf16[8,256,4,128]{1,3,2,0:T(8,128)(2,1)} %get-tuple-element.178, s32[]{:T(128)} %get-tuple-element.177, f32[4,256]{1,0:T(4,128)S(1)} %exponential_reduce_fusion.2, bf16[8,1280,128]{1,2,0:T(8,128)(2,1)} %get-tuple-element.190, pred[256,1280]{0,1:T(8,128)(4,1)S(1)} %compare_and_fusion.2, ...), kind=kOutput, calls=%fused_computation.10.clone.1 | convolution fusion | flops 677775616 | bytes 1513472 | tf_op jit(solution)/shard_map/while/body/eval_jaxpr/rqk,kd->qrd/dot_general | solution.py:41
  318.2 2.9 exponential_reduce_fusion.2
  321.1 4.2 %fusion.78 = bf16[8,256,4,128]{1,3,2,0:T(8,128)(2,1)} fusion(bf16[8,256,4,128]{1,3,2,0:T(8,128)(2,1)} %get-tuple-element.178, s32[]{:T(128)} %get-tuple-element.177, f32[4,256]{1,0:T(4,128)S(1)} %exponential_reduce_fusion.2, bf16[8,1280,128]{1,2,0:T(8,128)(2,1)} %get-tuple-element.190, pred[256,1280]{0,1:T(8,128)(4,1)S(1)} %compare_and_fusion.2, ...), kind=kOutput, calls=%fused_computation.10.clone.1 | convolution fusion | flops 677775616 | bytes 1513472 | tf_op jit(solution)/shard_map/while/body/eval_jaxpr/rqk,kd->qrd/dot_general | solution.py:41
  325.3 4.1 %copy.51 = bf16[1,256,4096]{2,1,0:T(8,128)(2,1)} copy(bf16[1,256,4096]{1,2,0:T(8,128)(2,1)} %bitcast.93) | data formatting | bytes 4194304 | tf_op jit(solution)/shard_map/reshape;reshape | solution.py:81
  (53 shorter events, 19.3 us)
Async XLA Ops:
  6.5 118.2 %copy-start = (bf16[1,256,5120]{2,1,0:T(8,128)(2,1)S(1)}, bf16[1,256,5120]{2,1,0:T(8,128)(2,1)}, u32[]{:S(2)}) copy-start(bf16[1,256,5120]{2,1,0:T(8,128)(2,1)} %param.8) | copy-start | bytes 7864324
  6.5 118.2 %copy-start.6 = (f32[5120]{0:T(1024)S(1)}, f32[5120]{0:T(1024)}, u32[]{:S(2)}) copy-start(f32[5120]{0:T(1024)} %param.10) | copy-start | bytes 61444
  6.5 118.2 %all-gather.2.cloned.1.call-start = ((), (), s32[]{:S(2)}) async-start(), calls=%async_computation | async-start | bytes 22282240 | tf_op jit(solution)/shard_map/all_gather | solution.py:58
  10.7 125.3 %copy-start.5 = (f32[1024]{0:T(1024)S(1)}, f32[1024]{0:T(1024)}, u32[]{:S(2)}) copy-start(f32[1024]{0:T(1024)} %param.12) | copy-start | bytes 12292
  134.6 1.3 copy-start.1
  136.0 10.8 %copy-start.2 = (f32[256,2048]{1,0:T(8,128)S(1)}, f32[256,2048]{1,0:T(8,128)}, u32[]{:S(2)}) copy-start(f32[256,2048]{1,0:T(8,128)} %copy-done.1) | copy-start | bytes 6291460
  136.3 17.8 %collective-permute-start = (bf16[256,8,128]{0,2,1:T(8,128)(2,1)S(1)}, bf16[256,8,128]{0,2,1:T(8,128)(2,1)}, u32[]{:S(2)}, u32[]{:S(2)}) collective-permute-start(bf16[256,8,128]{0,2,1:T(8,128)(2,1)S(1)} %bitcast.94), channel_id=1, source_target_pairs={{0,4},{1,5},{2,6},{3,7},{4,8},{5,9},{6,10},{7,11},{8,12},{9,13},{1... | collective-permute-start | bytes 1572872 | tf_op jit(solution)/shard_map/ppermute | solution.py:15
  137.7 54.5 %collective-permute-start.1 = (bf16[256,8,128]{0,2,1:T(8,128)(2,1)S(1)}, bf16[256,8,128]{0,2,1:T(8,128)(2,1)}, u32[]{:S(2)}, u32[]{:S(2)}) collective-permute-start(bf16[256,8,128]{0,2,1:T(8,128)(2,1)S(1)} %bitcast.95), channel_id=1, source_target_pairs={{0,3},{1,4},{2,5},{3,6},{4,7},{5,8},{6,9},{7,10},{8,11},{9,12},{10... | collective-permute-start | bytes 1572872 | tf_op jit(solution)/shard_map/ppermute | solution.py:15
  139.1 55.5 %collective-permute-start.2 = (bf16[256,8,128]{0,2,1:T(8,128)(2,1)S(1)}, bf16[256,8,128]{0,2,1:T(8,128)(2,1)}, u32[]{:S(2)}, u32[]{:S(2)}) collective-permute-start(bf16[256,8,128]{0,2,1:T(8,128)(2,1)S(1)} %bitcast.96), channel_id=1, source_target_pairs={{0,2},{1,3},{2,4},{3,5},{4,6},{5,7},{6,8},{7,9},{8,10},{9,11},{10,... | collective-permute-start | bytes 1572872 | tf_op jit(solution)/shard_map/ppermute | solution.py:15
  144.5 84.1 %collective-permute-start.3 = (bf16[256,8,128]{0,2,1:T(8,128)(2,1)S(1)}, bf16[256,8,128]{0,2,1:T(8,128)(2,1)S(1)}, u32[]{:S(2)}, u32[]{:S(2)}) collective-permute-start(bf16[256,8,128]{0,2,1:T(8,128)(2,1)S(1)} %bitcast.97), channel_id=1, source_target_pairs={{0,1},{1,2},{2,3},{3,4},{4,5},{5,6},{6,7},{7,8},{8,9},{9,10},{10,1... | collective-permute-start | bytes 1572872 | tf_op jit(solution)/shard_map/ppermute | solution.py:15
  147.0 81.8 %collective-permute-start.4 = (bf16[256,8,128]{2,0,1:T(8,128)(2,1)S(1)}, bf16[256,8,128]{2,0,1:T(8,128)(2,1)S(1)}, u32[]{:S(2)}, u32[]{:S(2)}) collective-permute-start(bf16[256,8,128]{2,0,1:T(8,128)(2,1)S(1)} %copy_bitcast_fusion), channel_id=1, source_target_pairs={{0,4},{1,5},{2,6},{3,7},{4,8},{5,9},{6,10},{7,11},{8,12},{9,13},{1... | collective-permute-start | bytes 1572872 | tf_op jit(solution)/shard_map/ppermute | solution.py:15
  154.0 74.7 %collective-permute-start.5 = (bf16[256,8,128]{2,0,1:T(8,128)(2,1)S(1)}, bf16[256,8,128]{2,0,1:T(8,128)(2,1)S(1)}, u32[]{:S(2)}, u32[]{:S(2)}) collective-permute-start(bf16[256,8,128]{2,0,1:T(8,128)(2,1)S(1)} %copy_bitcast_fusion), channel_id=1, source_target_pairs={{0,3},{1,4},{2,5},{3,6},{4,7},{5,8},{6,9},{7,10},{8,11},{9,12},{10... | collective-permute-start | bytes 1572872 | tf_op jit(solution)/shard_map/ppermute | solution.py:15
  192.3 42.8 %collective-permute-start.6 = (bf16[256,8,128]{2,0,1:T(8,128)(2,1)S(1)}, bf16[256,8,128]{2,0,1:T(8,128)(2,1)S(1)}, u32[]{:S(2)}, u32[]{:S(2)}) collective-permute-start(bf16[256,8,128]{2,0,1:T(8,128)(2,1)S(1)} %copy_bitcast_fusion), channel_id=1, source_target_pairs={{0,2},{1,3},{2,4},{3,5},{4,6},{5,7},{6,8},{7,9},{8,10},{9,11},{10,... | collective-permute-start | bytes 1572872 | tf_op jit(solution)/shard_map/ppermute | solution.py:15
  194.6 64.2 %collective-permute-start.7 = (bf16[256,8,128]{2,0,1:T(8,128)(2,1)S(1)}, bf16[256,8,128]{2,0,1:T(8,128)(2,1)S(1)}, u32[]{:S(2)}, u32[]{:S(2)}) collective-permute-start(bf16[256,8,128]{2,0,1:T(8,128)(2,1)S(1)} %copy_bitcast_fusion), channel_id=1, source_target_pairs={{0,1},{1,2},{2,3},{3,4},{4,5},{5,6},{6,7},{7,8},{8,9},{9,10},{10,1... | collective-permute-start | bytes 1572872 | tf_op jit(solution)/shard_map/ppermute | solution.py:15
  228.7 30.3 %copy-start.3 = (bf16[1280,8,128]{0,2,1:T(8,128)(2,1)}, bf16[1280,8,128]{0,2,1:T(8,128)(2,1)S(1)}, u32[]{:S(2)}) copy-start(bf16[1280,8,128]{0,2,1:T(8,128)(2,1)S(1)} %constant_dynamic-update-slice_fusion) | copy-start | bytes 7864324
  259.1 1.5 copy-start.4
Sparse Core Ops, SparseCore 0:
  9.2 115.4 all-gather.1
where the time goes:
time: 337 us; the launch traced here: 336 us
  waiting for transfers between devices  186 us (55%)
  matrix products  66.3 us (20%)
  starting transfers between devices  43.1 us (13%)
  local copies, waits for them, and re-layouts  15.8 us (5%)
  between operations  13.7 us (4%)
  other arithmetic  11 us (3%)
    all_gather x1, waiting for transfers between devices, shards(): lax.all_gather(kv_weight, 'fsdp', axis=0, tiled=True)  114 us
    ppermute x8, waiting for transfers between devices, from_behind(): return lax.ppermute(value, axis, pairs)  71.5 us
    ppermute x8, starting transfers between devices, from_behind(): return lax.ppermute(value, axis, pairs)  43.1 us
    dot_general x8, matrix products, one_group(): jnp.einsum('rqk,kd->qrd', probs, value_one, preferred_element_type=jnp.fl...  33.3 us
    sub x8, matrix products, one_group(): probs = jnp.exp(scores - highest)  23.1 us
    unnamed x23, local copies, waits for them, and re-layouts  10.5 us
    dot_general x1, matrix products, shards(): jnp.dot(normed, lax.all_gather(kv_weight, 'fsdp', axis=0, tiled=True), pr...  9.9 us
    and x8, other arithmetic, attend_near(): (key_pos[None, :] >= 0) & (key_pos[None, :] <= query_pos[:, None])  8.24 us
  transfers between devices with their start and end apart: 9, of which 5 were waited for; matrix products, arithmetic and copies ran while one was open for 3% of the time, Pallas kernels for 0%

commit v1 on v0

--- a/solution.py
+++ b/solution.py
@@ -7,6 +7,11 @@
 KVH = 8
 HD = 128
 EPS = 1e-06
+
+
+def swapped_in(x, name, d):
+    sent = jnp.stack([x] * lax.axis_size(name))
+    return jnp.concatenate(lax.all_to_all(sent, name, 0, 0), axis=d)
 
 
 def from_behind(value, axis, by):
@@ -54,9 +59,7 @@
         wide * lax.rsqrt(jnp.mean(wide * wide, axis=-1, keepdims=True) + EPS) * norm_gain
     ).astype(jnp.bfloat16)
     projected = jnp.dot(
-        normed,
-        lax.all_gather(kv_weight, "fsdp", axis=0, tiled=True),
-        preferred_element_type=jnp.float32,
+        normed, swapped_in(kv_weight, "fsdp", 0), preferred_element_type=jnp.float32
     )
     keys = projected[:, : KVH * HD].astype(jnp.bfloat16).reshape(token_count, KVH, HD)
     values = (

time: 337 us -> 450 us (1.34)
  waiting for transfers between devices: 186 us -> 277 us
  starting transfers between devices: 43.1 us -> 72.6 us
  between operations: 13.7 us -> 0.3 us
  local copies, waits for them, and re-layouts: 15.8 us -> 23.3 us
    all_to_all x0 -> x1, waiting for transfers between devices: none -> 228 us  [swapped_in(): return jnp.concatenate(lax.all_to_all(sent, name, 0, 0), axis=d)]
    all_gather x1 -> x0, waiting for transfers between devices: 114 us -> none  [shards(): lax.all_gather(kv_weight, 'fsdp', axis=0, tiled=True)]
    ppermute x8, starting transfers between devices: 43.1 us -> 66.6 us  [from_behind(): return lax.ppermute(value, axis, pairs)]
    ppermute x8, waiting for transfers between devices: 71.5 us -> 48.4 us  [from_behind(): return lax.ppermute(value, axis, pairs)]
    another operation x1 -> x2, local copies, waits for them, and re-layouts: 0.81 us -> 8.31 us  [the longest x1 8.23 us: swapped_in(): sent = jnp.stack([x] * lax.axis_size(name))]
    all_to_all x0 -> x1, starting transfers between devices: none -> 6 us  [swapped_in(): return jnp.concatenate(lax.all_to_all(sent, name, 0, 0), axis=d)]
    unnamed x23 -> x25, local copies, waits for them, and re-layouts: 10.5 us -> 10.5 us
  transfers between devices with their start and end apart: 9 -> 9, of which waited for: 5 -> 5; matrix products, arithmetic and copies ran while one was open for 3% -> 2% of each run, Pallas kernels for 0% -> 0%
where the time goes in v1:
time: 450 us; the launch traced here: 449 us
  waiting for transfers between devices  277 us (62%)
  starting transfers between devices  72.6 us (16%)
  matrix products  66.3 us (15%)
  local copies, waits for them, and re-layouts  23.3 us (5%)
  other arithmetic  9.31 us (2%)
    all_to_all x1, waiting for transfers between devices, swapped_in(): return jnp.concatenate(lax.all_to_all(sent, name, 0, 0), axis=d)  228 us
    ppermute x8, starting transfers between devices, from_behind(): return lax.ppermute(value, axis, pairs)  66.6 us
    ppermute x8, waiting for transfers between devices, from_behind(): return lax.ppermute(value, axis, pairs)  48.4 us
    dot_general x8, matrix products, one_group(): jnp.einsum('rqk,kd->qrd', probs, value_one, preferred_element_type=jnp.fl...  33.3 us
    sub x8, matrix products, one_group(): probs = jnp.exp(scores - highest)  23.1 us
    unnamed x25, local copies, waits for them, and re-layouts  10.5 us
    dot_general x1, matrix products, shards(): jnp.dot(normed, swapped_in(kv_weight, 'fsdp', 0), preferred_element_type=...  9.91 us
  transfers between devices with their start and end apart: 9, of which 5 were waited for; matrix products, arithmetic and copies ran while one was open for 2% of the time, Pallas kernels for 0%

profile of v1, /device:TPU:135, one launch (start us, length us, event | category | flops | bytes accessed | tf_op | source)
XLA Modules:
  0.0 448.7 jit_solution(5534120897545802778)
XLA Ops:
  0.0 8.2 %stack.2 = bf16[16,320,2048]{2,1,0:T(8,128)(2,1)} broadcast(bf16[320,2048]{1,0:T(8,128)(2,1)} %param.11), dimensions={1,2} | broadcast | bytes 22282240 | tf_op jit(solution)/shard_map/stack | solution.py:13
  8.2 6.0 %all-to-all-start = ((bf16[16,320,2048]{2,1,0:T(8,128)(2,1)}), bf16[16,320,2048]{2,1,0:T(8,128)(2,1)}, u32[]{:S(2)}, u32[]{:S(2)}) async-start(bf16[16,320,2048]{2,1,0:T(8,128)(2,1)} %stack.2), calls=%async_computation | async-start | bytes 41943040 | tf_op jit(solution)/shard_map/all_to_all | solution.py:14
  15.2 228.4 %all-to-all-done = bf16[16,320,2048]{2,1,0:T(8,128)(2,1)} async-done(((bf16[16,320,2048]{2,1,0:T(8,128)(2,1)}), bf16[16,320,2048]{2,1,0:T(8,128)(2,1)}, u32[]{:S(2)}, u32[]{:S(2)}) %all-to-all-start) | async-done | bytes 20971552 | tf_op jit(solution)/shard_map/all_to_all | solution.py:14
  243.6 9.9 %fusion.54 = f32[256,2048]{1,0:T(8,128)S(1)} fusion(bf16[5120,2048]{1,0:T(8,128)(2,1)} %bitcast.1, bf16[1,256,5120]{2,1,0:T(8,128)(2,1)S(1)} %copy-done, f32[5120]{0:T(1024)S(1)} %copy-done.7, f32[256]{0:T(256)S(1)} %add_rsqrt_fusion), kind=kOutput, calls=%fused_computation.38 | convolution fusion | flops 5373952000 | bytes 25711616 | tf_op jit(solution)/shard_map/dot_general | solution.py:61
  253.6 1.3 copy-done.1
  255.2 1.4 collective-permute-start
  259.3 4.1 copy.46
  263.4 3.1 collective-permute-start.3
  267.9 7.0 %collective-permute-done = bf16[256,8,128]{0,2,1:T(8,128)(2,1)} collective-permute-done((bf16[256,8,128]{0,2,1:T(8,128)(2,1)S(1)}, bf16[256,8,128]{0,2,1:T(8,128)(2,1)}, u32[]{:S(2)}, u32[]{:S(2)}) %collective-permute-start) | collective-permute-done | bytes 524320 | tf_op jit(solution)/shard_map/ppermute | solution.py:20
  277.3 11.4 %collective-permute-done.1 = bf16[256,8,128]{0,2,1:T(8,128)(2,1)} collective-permute-done((bf16[256,8,128]{0,2,1:T(8,128)(2,1)S(1)}, bf16[256,8,128]{0,2,1:T(8,128)(2,1)}, u32[]{:S(2)}, u32[]{:S(2)}) %collective-permute-start.1) | collective-permute-done | bytes 524320 | tf_op jit(solution)/shard_map/ppermute | solution.py:20
  291.1 55.7 %collective-permute-start.7 = (bf16[256,8,128]{2,0,1:T(8,128)(2,1)S(1)}, bf16[256,8,128]{2,0,1:T(8,128)(2,1)S(1)}, u32[]{:S(2)}, u32[]{:S(2)}) collective-permute-start(bf16[256,8,128]{2,0,1:T(8,128)(2,1)S(1)} %copy_bitcast_fusion), channel_id=1, source_target_pairs={{0,1},{1,2},{2,3},{3,4},{4,5},{5,6},{6,7},{7,8},{8,9},{9,10},{10,1... | collective-permute-start | bytes 1572872 | tf_op jit(solution)/shard_map/ppermute | solution.py:20
  348.2 5.5 %collective-permute-done.6 = bf16[256,8,128]{2,0,1:T(8,128)(2,1)S(1)} collective-permute-done((bf16[256,8,128]{2,0,1:T(8,128)(2,1)S(1)}, bf16[256,8,128]{2,0,1:T(8,128)(2,1)S(1)}, u32[]{:S(2)}, u32[]{:S(2)}) %collective-permute-start.6) | collective-permute-done | bytes 524320 | tf_op jit(solution)/shard_map/ppermute | solution.py:20
  353.7 24.4 %collective-permute-done.7 = bf16[256,8,128]{2,0,1:T(8,128)(2,1)S(1)} collective-permute-done((bf16[256,8,128]{2,0,1:T(8,128)(2,1)S(1)}, bf16[256,8,128]{2,0,1:T(8,128)(2,1)S(1)}, u32[]{:S(2)}, u32[]{:S(2)}) %collective-permute-start.7) | collective-permute-done | bytes 524320 | tf_op jit(solution)/shard_map/ppermute | solution.py:20
  378.3 1.5 copy-done.4
  379.9 64.7 %while.11 = (s32[]{:T(128)}, bf16[8,256,4,128]{1,3,2,0:T(8,128)(2,1)}, bf16[8,1280,128]{1,2,0:T(8,128)(2,1)}, bf16[8,1280,128]{2,1,0:T(8,128)(2,1)}, bf16[8,256,...) while((s32[]{:T(128)}, ...), condition=%wide.region_7.8_spmd.clone, body=%wide.region_4.7_spmd.clone.sunk | while | flops 1019874816 | bytes 2777453 | solution.py:49
  380.9 2.9 exponential_reduce_fusion.2
  383.8 4.2 fusion.78
  389.0 2.9 exponential_reduce_fusion.2
  391.9 4.1 fusion.78
  397.1 2.9 exponential_reduce_fusion.2
  399.9 4.1 fusion.78
  405.1 2.9 exponential_reduce_fusion.2
  408.0 4.2 fusion.78
  413.2 2.9 exponential_reduce_fusion.2
  416.1 4.2 fusion.78
  421.3 2.9 exponential_reduce_fusion.2
  424.2 4.2 fusion.78
  429.4 2.9 exponential_reduce_fusion.2
  432.3 4.2 fusion.78
  437.5 2.9 exponential_reduce_fusion.2
  440.4 4.2 fusion.78
  444.6 4.1 copy.51
  (55 shorter events, 19.8 us)
Async XLA Ops:
  8.2 6.0 %copy-start.6 = (s32[1,16]{1,0:T(1,128)S(1)}, s32[1,16]{1,0:T(1,128)}, u32[]{:S(2)}) copy-start(s32[1,16]{1,0:T(1,128)} %param.13) | copy-start | bytes 196
  8.2 6.4 %copy-start = (bf16[1,256,5120]{2,1,0:T(8,128)(2,1)S(1)}, bf16[1,256,5120]{2,1,0:T(8,128)(2,1)}, u32[]{:S(2)}) copy-start(bf16[1,256,5120]{2,1,0:T(8,128)(2,1)} %param.8) | copy-start | bytes 7864324
  8.2 235.4 %all-to-all-start = ((bf16[16,320,2048]{2,1,0:T(8,128)(2,1)}), bf16[16,320,2048]{2,1,0:T(8,128)(2,1)}, u32[]{:S(2)}, u32[]{:S(2)}) async-start(bf16[16,320,2048]{2,1,0:T(8,128)(2,1)} %stack.2), calls=%async_computation | async-start | bytes 41943040 | tf_op jit(solution)/shard_map/all_to_all | solution.py:14
  14.2 229.4 %copy-start.7 = (f32[5120]{0:T(1024)S(1)}, f32[5120]{0:T(1024)}, u32[]{:S(2)}) copy-start(f32[5120]{0:T(1024)} %param.10) | copy-start | bytes 61444
  243.6 11.2 %copy-start.5 = (f32[1024]{0:T(1024)S(1)}, f32[1024]{0:T(1024)}, u32[]{:S(2)}) copy-start(f32[1024]{0:T(1024)} %param.12) | copy-start | bytes 12292
  253.5 1.3 copy-start.1
  255.0 11.6 %copy-start.2 = (f32[256,2048]{1,0:T(8,128)S(1)}, f32[256,2048]{1,0:T(8,128)}, u32[]{:S(2)}) copy-start(f32[256,2048]{1,0:T(8,128)} %copy-done.1) | copy-start | bytes 6291460
  255.2 19.7 %collective-permute-start = (bf16[256,8,128]{0,2,1:T(8,128)(2,1)S(1)}, bf16[256,8,128]{0,2,1:T(8,128)(2,1)}, u32[]{:S(2)}, u32[]{:S(2)}) collective-permute-start(bf16[256,8,128]{0,2,1:T(8,128)(2,1)S(1)} %bitcast.91), channel_id=1, source_target_pairs={{0,4},{1,5},{2,6},{3,7},{4,8},{5,9},{6,10},{7,11},{8,12},{9,13},{1... | collective-permute-start | bytes 1572872 | tf_op jit(solution)/shard_map/ppermute | solution.py:20
  256.6 32.1 %collective-permute-start.1 = (bf16[256,8,128]{0,2,1:T(8,128)(2,1)S(1)}, bf16[256,8,128]{0,2,1:T(8,128)(2,1)}, u32[]{:S(2)}, u32[]{:S(2)}) collective-permute-start(bf16[256,8,128]{0,2,1:T(8,128)(2,1)S(1)} %bitcast.92), channel_id=1, source_target_pairs={{0,3},{1,4},{2,5},{3,6},{4,7},{5,8},{6,9},{7,10},{8,11},{9,12},{10... | collective-permute-start | bytes 1572872 | tf_op jit(solution)/shard_map/ppermute | solution.py:20
  258.0 33.1 %collective-permute-start.2 = (bf16[256,8,128]{0,2,1:T(8,128)(2,1)S(1)}, bf16[256,8,128]{0,2,1:T(8,128)(2,1)}, u32[]{:S(2)}, u32[]{:S(2)}) collective-permute-start(bf16[256,8,128]{0,2,1:T(8,128)(2,1)S(1)} %bitcast.93), channel_id=1, source_target_pairs={{0,2},{1,3},{2,4},{3,5},{4,6},{5,7},{6,8},{7,9},{8,10},{9,11},{10,... | collective-permute-start | bytes 1572872 | tf_op jit(solution)/shard_map/ppermute | solution.py:20
  263.4 84.5 %collective-permute-start.3 = (bf16[256,8,128]{0,2,1:T(8,128)(2,1)S(1)}, bf16[256,8,128]{0,2,1:T(8,128)(2,1)S(1)}, u32[]{:S(2)}, u32[]{:S(2)}) collective-permute-start(bf16[256,8,128]{0,2,1:T(8,128)(2,1)S(1)} %bitcast.94), channel_id=1, source_target_pairs={{0,1},{1,2},{2,3},{3,4},{4,5},{5,6},{6,7},{7,8},{8,9},{9,10},{10,1... | collective-permute-start | bytes 1572872 | tf_op jit(solution)/shard_map/ppermute | solution.py:20
  266.6 81.4 %collective-permute-start.4 = (bf16[256,8,128]{2,0,1:T(8,128)(2,1)S(1)}, bf16[256,8,128]{2,0,1:T(8,128)(2,1)S(1)}, u32[]{:S(2)}, u32[]{:S(2)}) collective-permute-start(bf16[256,8,128]{2,0,1:T(8,128)(2,1)S(1)} %copy_bitcast_fusion), channel_id=1, source_target_pairs={{0,4},{1,5},{2,6},{3,7},{4,8},{5,9},{6,10},{7,11},{8,12},{9,13},{1... | collective-permute-start | bytes 1572872 | tf_op jit(solution)/shard_map/ppermute | solution.py:20
  274.9 73.1 %collective-permute-start.5 = (bf16[256,8,128]{2,0,1:T(8,128)(2,1)S(1)}, bf16[256,8,128]{2,0,1:T(8,128)(2,1)S(1)}, u32[]{:S(2)}, u32[]{:S(2)}) collective-permute-start(bf16[256,8,128]{2,0,1:T(8,128)(2,1)S(1)} %copy_bitcast_fusion), channel_id=1, source_target_pairs={{0,3},{1,4},{2,5},{3,6},{4,7},{5,8},{6,9},{7,10},{8,11},{9,12},{10... | collective-permute-start | bytes 1572872 | tf_op jit(solution)/shard_map/ppermute | solution.py:20
  288.7 64.9 %collective-permute-start.6 = (bf16[256,8,128]{2,0,1:T(8,128)(2,1)S(1)}, bf16[256,8,128]{2,0,1:T(8,128)(2,1)S(1)}, u32[]{:S(2)}, u32[]{:S(2)}) collective-permute-start(bf16[256,8,128]{2,0,1:T(8,128)(2,1)S(1)} %copy_bitcast_fusion), channel_id=1, source_target_pairs={{0,2},{1,3},{2,4},{3,5},{4,6},{5,7},{6,8},{7,9},{8,10},{9,11},{10,... | collective-permute-start | bytes 1572872 | tf_op jit(solution)/shard_map/ppermute | solution.py:20
  291.1 87.0 %collective-permute-start.7 = (bf16[256,8,128]{2,0,1:T(8,128)(2,1)S(1)}, bf16[256,8,128]{2,0,1:T(8,128)(2,1)S(1)}, u32[]{:S(2)}, u32[]{:S(2)}) collective-permute-start(bf16[256,8,128]{2,0,1:T(8,128)(2,1)S(1)} %copy_bitcast_fusion), channel_id=1, source_target_pairs={{0,1},{1,2},{2,3},{3,4},{4,5},{5,6},{6,7},{7,8},{8,9},{9,10},{10,1... | collective-permute-start | bytes 1572872 | tf_op jit(solution)/shard_map/ppermute | solution.py:20
  348.0 30.3 %copy-start.3 = (bf16[1280,8,128]{0,2,1:T(8,128)(2,1)}, bf16[1280,8,128]{0,2,1:T(8,128)(2,1)S(1)}, u32[]{:S(2)}) copy-start(bf16[1280,8,128]{0,2,1:T(8,128)(2,1)S(1)} %constant_dynamic-update-slice_fusion) | copy-start | bytes 7864324
  378.3 1.5 copy-start.4
